TPU v7x, 32 devices: a whole 2x2x4 slice. The times are simulated.
32 devices in a mesh: rows: 4 (over z), cx: 2 (over y), cy: 4 (over x, core).
Axes of the slice: x: 2, y: 2, z: 4, core: 2. Of those that a mesh axis runs over, the one named last changes fastest.
Arguments:
- rows_data: float32 [2048, 1024], P(('rows', 'cx', 'cy')), may hold values from -6 to 6
- owner_rows: int32 [2048, 1], P(('rows', 'cx', 'cy')), may hold values from 0 to 7; in each aligned block of 64 rows (0 to 63, 64 to 127, ...) at most 16 rows name the same one
- slot_rows: int32 [2048], P(('rows', 'cx', 'cy')), may hold values from 0 to 2047
- centroids: float32 [16384, 1024], P(('cx', 'cy'), 'rows'), may hold values from -6 to 6
- counts: float32 [16384], P(('cx', 'cy')), may hold values from 1 to 100
- owner_cent: int32 [16384, 1], P(('cx', 'cy')), may hold values from 0 to 7; in each aligned block of 2048 rows (0 to 2047, 2048 to 4095, ...) at most 512 rows name the same one
- slot_cent: int32 [16384], P(('cx', 'cy')), may hold values from 0 to 511
- upper: float32 [4096, 1024], P(('cx', 'cy'), 'rows'), may hold values from -6 to 6
- upper_counts: float32 [4096], P(('cx', 'cy')), may hold values from 1 to 100
Outputs:
- moved: float32 [16384, 1024], P(('cx', 'cy'), 'rows')
- new_counts: float32 [16384], P(('cx', 'cy'))
- new_upper: float32 [4096, 1024], P(('cx', 'cy'), 'rows')
- new_upper_counts: float32 [4096], P(('cx', 'cy'))
Inputs may be any that keep to these rules, and one draw needn't show every extreme that they name: `owner_rows`: the rows of one device name each value at most 16 times, and some device reaches it. `owner_cent`: the 2048 level-1 centroids of one shard name each value at most 512 times, and some shard reaches it.
All inputs are finite; a program needn't handle non-finite values.
Results may differ from a plain program's by a relative error of at most 0.00002.
Values sent between devices are 32-bit elements; how exact they have to be, the bound alone decides.
A program may use at most 64 MiB of HBM per device.

v0:
```python
import jax
import jax.numpy as jnp
from jax import lax
from jax.sharding import PartitionSpec as P


def bucket(values, owners, slot_ids, shards, capacity, empty):
    onehot = (owners[:, None] == jnp.arange(shards, dtype=jnp.int32)[None, :]).astype(jnp.int32)
    earlier = jnp.cumsum(onehot, axis=0) - onehot
    position = jnp.sum(earlier * onehot, axis=1)
    target = owners * capacity + position
    buffer = jnp.zeros((shards * capacity, values.shape[1]), values.dtype).at[target].set(values)
    labels = jnp.full((shards * capacity,), empty, jnp.int32).at[target].set(slot_ids)
    return (buffer.reshape(shards, capacity, values.shape[1]), labels.reshape(shards, capacity))


def accumulate(values, labels, segments):
    summed = jnp.zeros((segments, values.shape[1]), jnp.float32).at[labels].add(values, mode="drop")
    member_counts = (
        jnp.zeros((segments,), jnp.float32)
        .at[labels]
        .add(jnp.ones(labels.shape, jnp.float32), mode="drop")
    )
    return (summed, member_counts)


def damped(previous, weights, summed, member_counts):
    denominator = weights + member_counts
    updated = previous + (summed - member_counts[:, None] * previous) / denominator[:, None]
    return (updated, denominator)


def body(
    rows_data, owner_rows, slot_rows, centroids, counts, owner_cent, slot_cent, upper, upper_counts
):
    shards = lax.axis_size(("cx", "cy"))
    groups = lax.axis_size("rows")
    batch = rows_data.shape[0]
    lower_rows = centroids.shape[0]
    capacity = 2 * batch // shards
    buffer, labels = bucket(rows_data, owner_rows[:, 0], slot_rows, shards, capacity, lower_rows)
    labels = jnp.broadcast_to(labels[:, :, None], (shards, capacity, groups))
    arrived, arrived_labels = (
        lax.all_to_all(
            lax.all_to_all(buffer, "rows", split_axis=2, concat_axis=1, tiled=True),
            ("cx", "cy"),
            split_axis=0,
            concat_axis=0,
            tiled=True,
        ),
        lax.all_to_all(
            lax.all_to_all(labels, "rows", split_axis=2, concat_axis=1, tiled=True),
            ("cx", "cy"),
            split_axis=0,
            concat_axis=0,
            tiled=True,
        ),
    )
    slice_width = arrived.shape[2]
    summed, member_counts = accumulate(
        arrived.reshape(-1, slice_width), arrived_labels.reshape(-1), lower_rows
    )
    moved, new_counts = damped(centroids, counts, summed, member_counts)
    upper_rows = upper.shape[0]
    owners_upper = owner_cent[:, 0]
    labels_upper = owners_upper * upper_rows + slot_cent
    whole_partial, hit_counts = accumulate(moved, labels_upper, upper_rows * shards)
    upper_summed = lax.psum_scatter(whole_partial, ("cx", "cy"), scatter_dimension=0, tiled=True)
    upper_members = lax.psum_scatter(hit_counts, ("cx", "cy"), scatter_dimension=0, tiled=True)
    new_upper, new_upper_counts = damped(upper, upper_counts, upper_summed, upper_members)
    return (moved, new_counts, new_upper, new_upper_counts)


def solution(mesh):
    placed = (
        P(("rows", "cx", "cy"), None),
        P(("rows", "cx", "cy"), None),
        P(("rows", "cx", "cy")),
        P(("cx", "cy"), "rows"),
        P(("cx", "cy")),
        P(("cx", "cy"), None),
        P(("cx", "cy")),
        P(("cx", "cy"), "rows"),
        P(("cx", "cy")),
    )
    return jax.shard_map(
        body,
        mesh=mesh,
        in_specs=placed,
        out_specs=(
            P(("cx", "cy"), "rows"),
            P(("cx", "cy")),
            P(("cx", "cy"), "rows"),
            P(("cx", "cy")),
        ),
        check_vma=False,
    )
```

profile of v0, /device:TPU:0, one launch (start us, length us, event | category | flops | bytes accessed | tf_op | source)
XLA Modules:
  0.0 151.4 jit_solution(6357609695715163591)
XLA Ops:
  7.2 0.7 fusion.6
  7.9 0.1 reduce_window_sum.11
  8.0 0.8 select_reduce_fusion
  8.8 0.7 fusion.11
  9.5 0.9 scatter_custom_fusion
  10.4 0.1 broadcast_in_dim.46
  10.5 0.7 reshape.128
  11.2 6.3 %all-to-all-start = ((s32[4,1,128]{2,1,0:T(1,128)}), s32[4,1,128]{2,1,0:T(1,128)S(1)}, u32[]{:S(2)}, u32[]{:S(2)}) async-start(s32[4,1,128]{2,1,0:T(1,128)} %reshape.128), calls=%async_computation | async-start | bytes 4096 | tf_op jit(solution)/shard_map/all_to_all | solution.py:52
  17.5 1.4 scatter_custom_fusion.1
  18.9 2.6 %copy.16 = f32[8,16,1024]{1,0,2:T(8,128)} copy(f32[8,16,1024]{2,1,0:T(8,128)S(1)} %bitcast.33) | data formatting | bytes 1048576 | tf_op jit(solution)/shard_map/reshape | solution.py:14
  21.5 4.6 %reshape.130 = f32[4,1,32768]{2,1,0:T(1,128)} reshape(f32[1024,8,16]{2,1,0:T(8,128)} %bitcast.31) | data formatting | bytes 1048576
  26.1 0.0 all-to-all-done
  26.1 5.1 %all-to-all-start.2 = ((f32[4,1,32768]{2,1,0:T(1,128)}), f32[4,1,32768]{2,1,0:T(1,128)S(1)}, u32[]{:S(2)}, u32[]{:S(2)}) async-start(f32[4,1,32768]{2,1,0:T(1,128)} %reshape.130), calls=%async_computation.2 | async-start | bytes 1048576 | tf_op jit(solution)/shard_map/all_to_all | solution.py:45
  31.2 0.5 broadcast.64
  31.7 0.7 reduce.4
  32.4 0.1 reshape.129
  32.5 0.7 all_to_all.35
  33.1 12.0 %all-to-all-done.2 = f32[4,1,32768]{2,1,0:T(1,128)S(1)} async-done(((f32[4,1,32768]{2,1,0:T(1,128)}), f32[4,1,32768]{2,1,0:T(1,128)S(1)}, u32[]{:S(2)}, u32[]{:S(2)}) %all-to-all-start.2) | async-done | bytes 524320 | tf_op jit(solution)/shard_map/all_to_all | solution.py:45
  45.1 3.7 %all-to-all-start.1 = ((s32[8,64,1]{1,2,0:T(1,128)}), s32[8,64,1]{1,2,0:T(1,128)S(1)}, u32[]{:S(2)}, u32[]{:S(2)}) async-start(s32[8,64,1]{1,2,0:T(1,128)} %bitcast.5), calls=%async_computation.1 | async-start | bytes 8192 | tf_op jit(solution)/shard_map/all_to_all | solution.py:51
  48.8 0.5 broadcast.65
  49.3 2.1 %reduce.5 = f32[4,32768]{1,0:T(4,128)S(1)} reduce(f32[4,1,32768]{2,1,0:T(1,128)S(1)} %all-to-all-done.2, f32[]{:T(128)} %broadcast.65), dimensions={1}, to_apply=%all_to_all.37.reduce_sub_computation | reduce | bytes 1048580 | tf_op jit(solution)/shard_map/all_to_all | solution.py:45
  51.5 3.4 %reshape.131 = f32[1024,8,16]{2,1,0:T(8,128)} reshape(f32[4,32768]{1,0:T(4,128)S(1)} %reduce.5) | data formatting | bytes 1048576
  54.9 2.8 %copy.19 = f32[8,16,4,256]{3,2,1,0:T(4,128)S(1)} copy(f32[8,16,4,256]{1,0,3,2:T(8,128)} %bitcast.32) | data formatting | bytes 1048576 | tf_op jit(solution)/shard_map/all_to_all | solution.py:45
  57.7 0.0 copy-start.5
  57.7 0.0 copy-start.3
  57.8 0.0 copy-start.4
  57.8 0.9 copy.18
  58.7 0.0 all-to-all-done.1
  58.7 4.2 %all-to-all-start.3 = ((f32[8,64,256]{2,1,0:T(8,128)}), f32[8,64,256]{2,1,0:T(8,128)S(1)}, u32[]{:S(2)}, u32[]{:S(2)}) async-start(f32[8,64,256]{2,1,0:T(8,128)} %bitcast.10), calls=%async_computation.3 | async-start | bytes 1048576 | tf_op jit(solution)/shard_map/all_to_all | solution.py:44
  62.9 0.0 reduce-scatter.2.cloned.1.call-start
  63.0 0.5 broadcast.63
  63.5 0.7 reduce.3
  64.1 0.1 reshape.53
  64.2 3.2 %scatter_custom_fusion.3 = f32[2048]{0:T(1024)S(1)} fusion(s32[512]{0:T(512)S(1)} %bitcast.39, f32[512]{0:T(512)S(1)} %broadcast.51, f32[]{:T(128)} %constant.8.clone.1), kind=kCustom, calls=%fused_computation.22 | custom fusion | flops 512 | bytes 8196 | tf_op jit(solution)/shard_map/scatter-add | solution.py:22
  67.5 0.0 copy-start.1
  67.5 5.1 %all-to-all-done.3 = f32[8,64,256]{2,1,0:T(8,128)S(1)} async-done(((f32[8,64,256]{2,1,0:T(8,128)}), f32[8,64,256]{2,1,0:T(8,128)S(1)}, u32[]{:S(2)}, u32[]{:S(2)}) %all-to-all-start.3) | async-done | bytes 524320 | tf_op jit(solution)/shard_map/all_to_all | solution.py:44
  72.6 4.0 %scatter_custom_fusion.2 = f32[2048,256]{1,0:T(8,128)S(1)} fusion(s32[512]{0:T(512)S(1)} %bitcast.40, f32[512,256]{1,0:T(8,128)S(1)} %bitcast.35, f32[]{:T(128)} %constant.8.clone.1), kind=kCustom, calls=%fused_computation.9 | custom fusion | flops 131072 | bytes 2097156 | tf_op jit(solution)/shard_map/scatter-add | solution.py:18
  76.6 2.9 %divide_add_fusion = f32[2048,256]{1,0:T(8,128)} fusion(f32[2048,256]{1,0:T(8,128)} %param.12, f32[2048,256]{1,0:T(8,128)S(1)} %scatter_custom_fusion.2, f32[2048]{0:T(1024)S(1)} %add.54, f32[2048]{0:T(1024)S(1)} %scatter_custom_fusion.3), kind=kLoop, calls=%fused_computation.8 | loop fusion | flops 2097152 | bytes 6307840 | tf_op jit(solution)/shard_map/add | solution.py:29
  79.5 14.1 %scatter_custom_fusion.4 = f32[4096,256]{1,0:T(8,128)} fusion(s32[2048]{0:T(1024)S(1)} %compare_select_fusion, f32[2048,256]{1,0:T(8,128)} %divide_add_fusion, f32[]{:T(128)} %constant.8.clone.1), kind=kCustom, calls=%fused_computation.6 | custom fusion | flops 524288 | bytes 4194816 | tf_op jit(solution)/shard_map/scatter-add | solution.py:18
  93.6 0.0 reduce-scatter.2.cloned.1.call-update
  93.6 11.2 %scatter_custom_fusion.5 = f32[4096]{0:T(1024)S(1)} fusion(s32[2048]{0:T(1024)S(1)} %compare_select_fusion, f32[2048]{0:T(1024)S(1)} %broadcast.52, f32[]{:T(128)} %constant.8.clone.1), kind=kCustom, calls=%fused_computation.19 | custom fusion | flops 2048 | bytes 16388 | tf_op jit(solution)/shard_map/scatter-add | solution.py:22
  104.9 0.0 copy-done.7
  104.9 0.6 dynamic-slice
  106.2 23.2 %all-reduce = f32[4096]{0:T(1024)S(1)} all-reduce(f32[4096]{0:T(1024)S(1)} %scatter_custom_fusion.5), channel_id=3, replica_groups=mesh['rows'=4,'cx'=2,'cy'=4] {'cx','cy'}, use_global_device_ids=true, to_apply=%region_9.10.clone | all-reduce | flops 4096 | bytes 32768
  129.3 0.1 fusion.14
  129.4 13.1 %reduce-scatter.2.cloned.1.call-done = f32[512,256]{1,0:T(8,128)} async-done(((f32[4096,256]{1,0:T(8,128)}), f32[512,256]{1,0:T(8,128)}) %reduce-scatter.2.cloned.1.call-update) | async-done | bytes 524304 | tf_op jit(solution)/shard_map/reduce_scatter | solution.py:68
  142.5 2.0 %divide_add_fusion.1 = f32[512,256]{1,0:T(8,128)} fusion(f32[512,256]{1,0:T(8,128)S(1)} %copy-done, f32[512,256]{1,0:T(8,128)} %reduce-scatter.2.cloned.1.call-done, f32[512]{0:T(512)S(1)} %get-tuple-element.4, f32[512]{0:T(512)S(1)} %get-tuple-element.5), kind=kLoop, calls=%fused_computation.11 | loop fusion | flops 524288 | bytes 1576960 | tf_op jit(solution)/shard_map/add | solution.py:29
  144.5 0.0 copy-done.2
  (19 shorter events, 0.1 us)
Async XLA Ops:
  11.2 14.9 %all-to-all-start = ((s32[4,1,128]{2,1,0:T(1,128)}), s32[4,1,128]{2,1,0:T(1,128)S(1)}, u32[]{:S(2)}, u32[]{:S(2)}) async-start(s32[4,1,128]{2,1,0:T(1,128)} %reshape.128), calls=%async_computation | async-start | bytes 4096 | tf_op jit(solution)/shard_map/all_to_all | solution.py:52
  26.1 19.0 %all-to-all-start.2 = ((f32[4,1,32768]{2,1,0:T(1,128)}), f32[4,1,32768]{2,1,0:T(1,128)S(1)}, u32[]{:S(2)}, u32[]{:S(2)}) async-start(f32[4,1,32768]{2,1,0:T(1,128)} %reshape.130), calls=%async_computation.2 | async-start | bytes 1048576 | tf_op jit(solution)/shard_map/all_to_all | solution.py:45
  45.1 13.5 %all-to-all-start.1 = ((s32[8,64,1]{1,2,0:T(1,128)}), s32[8,64,1]{1,2,0:T(1,128)S(1)}, u32[]{:S(2)}, u32[]{:S(2)}) async-start(s32[8,64,1]{1,2,0:T(1,128)} %bitcast.5), calls=%async_computation.1 | async-start | bytes 8192 | tf_op jit(solution)/shard_map/all_to_all | solution.py:51
  57.7 5.2 %copy-start.5 = (s32[2048,1]{0,1:T(1,128)S(1)}, s32[2048,1]{0,1:T(1,128)}, u32[]{:S(2)}) copy-start(s32[2048,1]{0,1:T(1,128)} %param.14) | copy-start | bytes 24580
  57.7 5.2 %copy-start.3 = (s32[2048]{0:T(1024)S(1)}, s32[2048]{0:T(1024)}, u32[]{:S(2)}) copy-start(s32[2048]{0:T(1024)} %param.15) | copy-start | bytes 24580
  57.8 9.7 %copy-start.4 = (f32[2048]{0:T(1024)S(1)}, f32[2048]{0:T(1024)}, u32[]{:S(2)}) copy-start(f32[2048]{0:T(1024)} %param.13) | copy-start | bytes 24580
  58.7 13.9 %all-to-all-start.3 = ((f32[8,64,256]{2,1,0:T(8,128)}), f32[8,64,256]{2,1,0:T(8,128)S(1)}, u32[]{:S(2)}, u32[]{:S(2)}) async-start(f32[8,64,256]{2,1,0:T(8,128)} %bitcast.10), calls=%async_computation.3 | async-start | bytes 1048576 | tf_op jit(solution)/shard_map/all_to_all | solution.py:44
  62.9 79.6 %reduce-scatter.2.cloned.1.call-start = ((), (), s32[]{:S(2)}) async-start(), calls=%async_computation.5 | async-start | bytes 4718592 | tf_op jit(solution)/shard_map/reduce_scatter | solution.py:68
  67.5 12.0 %copy-start.1 = (f32[2048]{0:T(1024)}, f32[2048]{0:T(1024)S(1)}, u32[]{:S(2)}) copy-start(f32[2048]{0:T(1024)S(1)} %add.54) | copy-start | bytes 24580
  93.6 11.3 %copy-start.7 = (u32[32]{0:T(128)S(1)}, u32[32]{0:T(128)}, u32[]{:S(2)}) copy-start(u32[32]{0:T(128)} %constant.5) | copy-start | bytes 388
  93.6 35.7 %copy-start.6 = (f32[512]{0:T(512)S(1)}, f32[512]{0:T(512)}, u32[]{:S(2)}) copy-start(f32[512]{0:T(512)} %param.17) | copy-start | bytes 6148
  93.6 48.9 %copy-start = (f32[512,256]{1,0:T(8,128)S(1)}, f32[512,256]{1,0:T(8,128)}, u32[]{:S(2)}) copy-start(f32[512,256]{1,0:T(8,128)} %param.16) | copy-start | bytes 1572868
  129.4 15.1 %copy-start.2 = (f32[512]{0:T(512)}, f32[512]{0:T(512)S(1)}, u32[]{:S(2)}) copy-start(f32[512]{0:T(512)S(1)} %get-tuple-element.4) | copy-start | bytes 6148
Sparse Core Ops, SparseCore 0:
  93.8 48.6 reduce-scatter.1
where the time goes:
time: 152 us; the launch traced here: 151 us
  other arithmetic  43.4 us (29%)
  waiting for transfers between devices  30.1 us (20%)
  blocking collectives  23.2 us (15%)
  local copies, waits for them, and re-layouts  20.4 us (13%)
  starting transfers between devices  19.4 us (13%)
  between operations  14.9 us (10%)
    unnamed x1, blocking collectives  23.2 us
    scatter-add x2, other arithmetic, accumulate(): jnp.zeros((segments, values.shape[1]), jnp.float32).at[labels]  18.1 us
    scatter-add x2, other arithmetic, accumulate(): member_counts = jnp.zeros((segments,), jnp.float32).at[labels].add(jnp.on...  14.5 us
    reduce_scatter x1, waiting for transfers between devices, body(): lax.psum_scatter(whole_partial, ('cx', 'cy'), scatter_dimension=0, tiled=...  13.1 us
    all_to_all x1, waiting for transfers between devices, body(): lax.all_to_all(buffer, 'rows', split_axis=2, concat_axis=1, tiled=True)  12 us
    unnamed x22, local copies, waits for them, and re-layouts  9.38 us
    all_to_all x1, starting transfers between devices, body(): lax.all_to_all(labels, 'rows', split_axis=2, concat_axis=1, tiled=True)  6.35 us
    all_to_all x1, starting transfers between devices, body(): lax.all_to_all(buffer, 'rows', split_axis=2, concat_axis=1, tiled=True)  5.09 us
  transfers between devices with their start and end apart: 5, of which 3 were waited for; matrix products, arithmetic and copies ran while one was open for 24% of the time, Pallas kernels for 0%

commit v1 on v0

--- a/solution.py
+++ b/solution.py
@@ -42,7 +42,12 @@
     labels = jnp.broadcast_to(labels[:, :, None], (shards, capacity, groups))
     arrived, arrived_labels = (
         lax.all_to_all(
-            lax.all_to_all(buffer, "rows", split_axis=2, concat_axis=1, tiled=True),
+            jnp.concatenate(
+                lax.all_to_all(
+                    jnp.stack(jnp.split(buffer, lax.axis_size("rows"), axis=2)), "rows", 0, 0
+                ),
+                axis=1,
+            ),
             ("cx", "cy"),
             split_axis=0,
             concat_axis=0,

time: 152 us -> 140 us (0.921)
  local copies, waits for them, and re-layouts: 20.4 us -> 6.4 us
  waiting for transfers between devices: 30.1 us -> 36.4 us
  starting transfers between devices: 19.4 us -> 17.1 us
    unnamed x22 -> x20, local copies, waits for them, and re-layouts: 9.38 us -> 1.38 us
    all_to_all x1, waiting for transfers between devices: 0.01 us -> 3.78 us  [body(): lax.all_to_all(lax.all_to_all(labels, 'rows', split_axis=2, concat_axis=1...]
    all_to_all x3 -> x1, local copies, waits for them, and re-layouts: 4.24 us -> 0.84 us  [body(): lax.all_to_all(jnp.stack(jnp.split(buffer, lax.axis_size('rows'), axis=2)...]
    all_to_all x1, waiting for transfers between devices: 0.01 us -> 3.21 us  [body(): lax.all_to_all(labels, 'rows', split_axis=2, concat_axis=1, tiled=True)]
    reshape x1 -> x0, local copies, waits for them, and re-layouts: 2.61 us -> none  [bucket(): buffer.reshape(shards, capacity, values.shape[1])]
    all_to_all x2, starting transfers between devices: 9.29 us -> 6.97 us  [the longest x1 3.49 us: body(): lax.all_to_all(jnp.concatenate(lax.all_to_all(jnp.stack(jnp.split(buffer,...]
    all_to_all x1 -> x0, other arithmetic: 2.14 us -> none  [body(): lax.all_to_all(buffer, 'rows', split_axis=2, concat_axis=1, tiled=True)]
  transfers between devices with their start and end apart: 5 -> 5, of which waited for: 3 -> 5; matrix products, arithmetic and copies ran while one was open for 24% -> 15% of each run, Pallas kernels for 0% -> 0%
where the time goes in v1:
time: 140 us
  other arithmetic  42 us (30%)
  waiting for transfers between devices  36.4 us (26%)
  blocking collectives  23.2 us (17%)
  starting transfers between devices  17.1 us (12%)
  between operations  14.9 us (11%)
  local copies, waits for them, and re-layouts  6.4 us (5%)
    unnamed x1, blocking collectives  23.2 us
    scatter-add x2, other arithmetic, accumulate(): jnp.zeros((segments, values.shape[1]), jnp.float32).at[labels]  17.9 us
    scatter-add x2, other arithmetic, accumulate(): member_counts = jnp.zeros((segments,), jnp.float32).at[labels].add(jnp.on...  14.5 us
    reduce_scatter x1, waiting for transfers between devices, body(): lax.psum_scatter(whole_partial, ('cx', 'cy'), scatter_dimension=0, tiled=...  13.1 us
    all_to_all x1, waiting for transfers between devices, body(): lax.all_to_all(jnp.stack(jnp.split(buffer, lax.axis_size('rows'), axis=2)...  11.4 us
    all_to_all x1, starting transfers between devices, body(): lax.all_to_all(labels, 'rows', split_axis=2, concat_axis=1, tiled=True)  6.35 us
    all_to_all x1, waiting for transfers between devices, body(): lax.all_to_all(jnp.concatenate(lax.all_to_all(jnp.stack(jnp.split(buffer,...  5 us
    add x2, other arithmetic, damped(): previous + (summed - member_counts[:, None] * previous) / denominator[:,...  4.95 us
  transfers between devices with their start and end apart: 5, of which 5 were waited for; matrix products, arithmetic and copies ran while one was open for 15% of the time, Pallas kernels for 0%

profile of v1, /device:TPU:0, one launch (start us, length us, event | category | flops | bytes accessed | tf_op | source)
XLA Modules:
  0.0 139.9 jit_solution(7597728511747641311)
XLA Ops:
  7.2 0.7 fusion.6
  7.9 0.1 reduce_window_sum.11
  8.0 0.8 select_reduce_fusion
  8.8 0.7 fusion.11
  9.5 0.9 scatter_custom_fusion
  10.4 0.1 broadcast_in_dim.46
  10.5 0.7 reshape.136
  11.2 6.3 %all-to-all-start = ((s32[4,1,128]{2,1,0:T(1,128)}), s32[4,1,128]{2,1,0:T(1,128)S(1)}, u32[]{:S(2)}, u32[]{:S(2)}) async-start(s32[4,1,128]{2,1,0:T(1,128)} %reshape.136), calls=%async_computation | async-start | bytes 4096 | tf_op jit(solution)/shard_map/all_to_all | solution.py:57
  17.5 1.4 scatter_custom_fusion.1
  18.9 0.1 slice_bitcast_fusion.3
  18.9 0.0 copy-start.5
  18.9 0.0 copy-start.3
  19.0 0.0 copy-start.4
  19.0 0.8 pad_maximum_fusion
  19.8 3.2 %all-to-all-done = s32[4,1,128]{2,1,0:T(1,128)S(1)} async-done(((s32[4,1,128]{2,1,0:T(1,128)}), s32[4,1,128]{2,1,0:T(1,128)S(1)}, u32[]{:S(2)}, u32[]{:S(2)}) %all-to-all-start) | async-done | bytes 2080 | tf_op jit(solution)/shard_map/all_to_all | solution.py:57
  23.0 3.5 %all-to-all-start.2 = ((f32[4,8,16,256]{3,2,1,0:T(8,128)}), f32[4,8,16,256]{3,2,1,0:T(8,128)S(1)}, u32[]{:S(2)}, u32[]{:S(2)}) async-start(f32[4,8,16,256]{3,2,1,0:T(8,128)} %pad_maximum_fusion), calls=%async_computation.2 | async-start | bytes 1048576 | tf_op jit(solution)/shard_map/all_to_all | solution.py:46
  26.5 0.5 broadcast.64
  27.0 0.7 reduce.4
  27.7 0.1 reshape.137
  27.8 0.7 all_to_all.25
  28.4 11.4 %all-to-all-done.2 = f32[4,8,16,256]{3,2,1,0:T(8,128)S(1)} async-done(((f32[4,8,16,256]{3,2,1,0:T(8,128)}), f32[4,8,16,256]{3,2,1,0:T(8,128)S(1)}, u32[]{:S(2)}, u32[]{:S(2)}) %all-to-all-start.2) | async-done | bytes 524320 | tf_op jit(solution)/shard_map/all_to_all | solution.py:46
  39.8 3.7 %all-to-all-start.1 = ((s32[8,64,1]{1,2,0:T(1,128)}), s32[8,64,1]{1,2,0:T(1,128)S(1)}, u32[]{:S(2)}, u32[]{:S(2)}) async-start(s32[8,64,1]{1,2,0:T(1,128)} %bitcast.5), calls=%async_computation.1 | async-start | bytes 8192 | tf_op jit(solution)/shard_map/all_to_all | solution.py:56
  43.5 0.8 copy.21
  44.4 3.8 %all-to-all-done.1 = s32[8,64,1]{1,2,0:T(1,128)S(1)} async-done(((s32[8,64,1]{1,2,0:T(1,128)}), s32[8,64,1]{1,2,0:T(1,128)S(1)}, u32[]{:S(2)}, u32[]{:S(2)}) %all-to-all-start.1) | async-done | bytes 2080 | tf_op jit(solution)/shard_map/all_to_all | solution.py:56
  48.1 3.5 %all-to-all-start.3 = ((f32[8,64,256]{2,1,0:T(8,128)}), f32[8,64,256]{2,1,0:T(8,128)S(1)}, u32[]{:S(2)}, u32[]{:S(2)}) async-start(f32[8,64,256]{2,1,0:T(8,128)} %bitcast.13), calls=%async_computation.3 | async-start | bytes 1048576 | tf_op jit(solution)/shard_map/all_to_all | solution.py:44
  51.6 0.0 reduce-scatter.2.cloned.1.call-start
  51.7 0.0 copy-done.5
  51.7 0.0 copy-done.3
  51.7 0.5 broadcast.63
  52.2 0.7 reduce.3
  52.9 0.1 reshape.59
  53.0 3.2 %scatter_custom_fusion.3 = f32[2048]{0:T(1024)S(1)} fusion(s32[512]{0:T(512)S(1)} %bitcast.42, f32[512]{0:T(512)S(1)} %broadcast.51, f32[]{:T(128)} %constant.8.clone.1), kind=kCustom, calls=%fused_computation.27 | custom fusion | flops 512 | bytes 8196 | tf_op jit(solution)/shard_map/scatter-add | solution.py:22
  56.2 0.0 copy-done.4
  56.3 0.0 copy-start.1
  56.3 5.0 %all-to-all-done.3 = f32[8,64,256]{2,1,0:T(8,128)S(1)} async-done(((f32[8,64,256]{2,1,0:T(8,128)}), f32[8,64,256]{2,1,0:T(8,128)S(1)}, u32[]{:S(2)}, u32[]{:S(2)}) %all-to-all-start.3) | async-done | bytes 524320 | tf_op jit(solution)/shard_map/all_to_all | solution.py:44
  61.3 3.8 %scatter_custom_fusion.2 = f32[2048,256]{1,0:T(8,128)S(1)} fusion(s32[512]{0:T(512)S(1)} %bitcast.43, f32[512,256]{1,0:T(8,128)S(1)} %bitcast.38, f32[]{:T(128)} %constant.8.clone.1), kind=kCustom, calls=%fused_computation.9 | custom fusion | flops 131072 | bytes 2097156 | tf_op jit(solution)/shard_map/scatter-add | solution.py:18
  65.1 2.9 %divide_add_fusion = f32[2048,256]{1,0:T(8,128)} fusion(f32[2048,256]{1,0:T(8,128)} %param.12, f32[2048,256]{1,0:T(8,128)S(1)} %scatter_custom_fusion.2, f32[2048]{0:T(1024)S(1)} %add.54, f32[2048]{0:T(1024)S(1)} %scatter_custom_fusion.3), kind=kLoop, calls=%fused_computation.8 | loop fusion | flops 2097152 | bytes 6307840 | tf_op jit(solution)/shard_map/add | solution.py:29
  68.0 0.0 copy-done.1
  68.0 14.1 %scatter_custom_fusion.4 = f32[4096,256]{1,0:T(8,128)} fusion(s32[2048]{0:T(1024)S(1)} %compare_select_fusion, f32[2048,256]{1,0:T(8,128)} %divide_add_fusion, f32[]{:T(128)} %constant.8.clone.1), kind=kCustom, calls=%fused_computation.6 | custom fusion | flops 524288 | bytes 4194816 | tf_op jit(solution)/shard_map/scatter-add | solution.py:18
  82.1 0.0 reduce-scatter.2.cloned.1.call-update
  82.2 11.2 %scatter_custom_fusion.5 = f32[4096]{0:T(1024)S(1)} fusion(s32[2048]{0:T(1024)S(1)} %compare_select_fusion, f32[2048]{0:T(1024)S(1)} %broadcast.52, f32[]{:T(128)} %constant.8.clone.1), kind=kCustom, calls=%fused_computation.24 | custom fusion | flops 2048 | bytes 16388 | tf_op jit(solution)/shard_map/scatter-add | solution.py:22
  93.4 0.6 dynamic-slice
  94.7 23.2 %all-reduce = f32[4096]{0:T(1024)S(1)} all-reduce(f32[4096]{0:T(1024)S(1)} %scatter_custom_fusion.5), channel_id=3, replica_groups=mesh['rows'=4,'cx'=2,'cy'=4] {'cx','cy'}, use_global_device_ids=true, to_apply=%region_9.10.clone | all-reduce | flops 4096 | bytes 32768
  117.9 0.1 fusion.14
  117.9 13.1 %reduce-scatter.2.cloned.1.call-done = f32[512,256]{1,0:T(8,128)} async-done(((f32[4096,256]{1,0:T(8,128)}), f32[512,256]{1,0:T(8,128)}) %reduce-scatter.2.cloned.1.call-update) | async-done | bytes 524304 | tf_op jit(solution)/shard_map/reduce_scatter | solution.py:73
  131.0 0.0 copy-done
  131.0 2.0 %divide_add_fusion.1 = f32[512,256]{1,0:T(8,128)} fusion(f32[512,256]{1,0:T(8,128)S(1)} %copy-done, f32[512,256]{1,0:T(8,128)} %reduce-scatter.2.cloned.1.call-done, f32[512]{0:T(512)S(1)} %get-tuple-element.4, f32[512]{0:T(512)S(1)} %get-tuple-element.5), kind=kLoop, calls=%fused_computation.12 | loop fusion | flops 524288 | bytes 1576960 | tf_op jit(solution)/shard_map/add | solution.py:29
  133.1 0.0 copy-done.2
  (15 shorter events, 0.1 us)
Async XLA Ops:
  11.2 11.8 %all-to-all-start = ((s32[4,1,128]{2,1,0:T(1,128)}), s32[4,1,128]{2,1,0:T(1,128)S(1)}, u32[]{:S(2)}, u32[]{:S(2)}) async-start(s32[4,1,128]{2,1,0:T(1,128)} %reshape.136), calls=%async_computation | async-start | bytes 4096 | tf_op jit(solution)/shard_map/all_to_all | solution.py:57
  18.9 32.8 %copy-start.5 = (s32[2048,1]{0,1:T(1,128)S(1)}, s32[2048,1]{0,1:T(1,128)}, u32[]{:S(2)}) copy-start(s32[2048,1]{0,1:T(1,128)} %param.14) | copy-start | bytes 24580
  18.9 32.8 %copy-start.3 = (s32[2048]{0:T(1024)S(1)}, s32[2048]{0:T(1024)}, u32[]{:S(2)}) copy-start(s32[2048]{0:T(1024)} %param.15) | copy-start | bytes 24580
  19.0 37.3 %copy-start.4 = (f32[2048]{0:T(1024)S(1)}, f32[2048]{0:T(1024)}, u32[]{:S(2)}) copy-start(f32[2048]{0:T(1024)} %param.13) | copy-start | bytes 24580
  23.0 16.8 %all-to-all-start.2 = ((f32[4,8,16,256]{3,2,1,0:T(8,128)}), f32[4,8,16,256]{3,2,1,0:T(8,128)S(1)}, u32[]{:S(2)}, u32[]{:S(2)}) async-start(f32[4,8,16,256]{3,2,1,0:T(8,128)} %pad_maximum_fusion), calls=%async_computation.2 | async-start | bytes 1048576 | tf_op jit(solution)/shard_map/all_to_all | solution.py:46
  39.8 8.3 %all-to-all-start.1 = ((s32[8,64,1]{1,2,0:T(1,128)}), s32[8,64,1]{1,2,0:T(1,128)S(1)}, u32[]{:S(2)}, u32[]{:S(2)}) async-start(s32[8,64,1]{1,2,0:T(1,128)} %bitcast.5), calls=%async_computation.1 | async-start | bytes 8192 | tf_op jit(solution)/shard_map/all_to_all | solution.py:56
  48.1 13.2 %all-to-all-start.3 = ((f32[8,64,256]{2,1,0:T(8,128)}), f32[8,64,256]{2,1,0:T(8,128)S(1)}, u32[]{:S(2)}, u32[]{:S(2)}) async-start(f32[8,64,256]{2,1,0:T(8,128)} %bitcast.13), calls=%async_computation.3 | async-start | bytes 1048576 | tf_op jit(solution)/shard_map/all_to_all | solution.py:44
  51.6 79.4 %reduce-scatter.2.cloned.1.call-start = ((), (), s32[]{:S(2)}) async-start(), calls=%async_computation.5 | async-start | bytes 4718592 | tf_op jit(solution)/shard_map/reduce_scatter | solution.py:73
  56.3 11.7 %copy-start.1 = (f32[2048]{0:T(1024)}, f32[2048]{0:T(1024)S(1)}, u32[]{:S(2)}) copy-start(f32[2048]{0:T(1024)S(1)} %add.54) | copy-start | bytes 24580
  82.1 11.3 %copy-start.7 = (u32[32]{0:T(128)S(1)}, u32[32]{0:T(128)}, u32[]{:S(2)}) copy-start(u32[32]{0:T(128)} %constant.5) | copy-start | bytes 388
  82.1 35.7 %copy-start.6 = (f32[512]{0:T(512)S(1)}, f32[512]{0:T(512)}, u32[]{:S(2)}) copy-start(f32[512]{0:T(512)} %param.17) | copy-start | bytes 6148
  82.1 48.9 %copy-start = (f32[512,256]{1,0:T(8,128)S(1)}, f32[512,256]{1,0:T(8,128)}, u32[]{:S(2)}) copy-start(f32[512,256]{1,0:T(8,128)} %param.16) | copy-start | bytes 1572868
  117.9 15.1 %copy-start.2 = (f32[512]{0:T(512)}, f32[512]{0:T(512)S(1)}, u32[]{:S(2)}) copy-start(f32[512]{0:T(512)S(1)} %get-tuple-element.4) | copy-start | bytes 6148
Sparse Core Ops, SparseCore 0:
  82.3 48.6 reduce-scatter.1
